TPU v7x, 32 devices: a whole 2x2x4 slice. The times are simulated.
32 devices in a mesh: feat: 8 (over y, x, core), rep: 4 (over z).
Axes of the slice: x: 2, y: 2, z: 4, core: 2. Of those that a mesh axis runs over, the one named last changes fastest.
Arguments:
- features: bfloat16 [4, 8, 1024, 512], P('rep', None, 'feat'), may hold values from -6 to 6
- adjacency_one: int32 [4, 8, 5, 16, 512], P('rep'), may hold values from 0 to 65535, as said below
- pre_hidden: bfloat16 [4, 8, 256, 256], P('rep', 'feat'), may hold values from -6 to 6
- adjacency_two: int32 [4, 8, 5, 8, 256], P('rep', 'feat'), may hold values from 0 to 65535, as said below
- weight_two: bfloat16 [6, 256, 256], replicated, may hold values from -0.375 to 0.375
- out_grad: bfloat16 [4, 8, 128, 256], P('rep', 'feat'), may hold values from -6 to 6
Outputs:
- grad_w1: float32 [6, 1024, 256], P(None, 'feat')
- grad_b1: float32 [256], replicated
- grad_w2: float32 [6, 256, 256], replicated
- grad_b2: float32 [256], replicated
Inputs may be any that keep to these rules, and one draw needn't show every extreme that they name: `adjacency_one`: bit k, k below 16, of word (w, n) is the entry of destination row 16 w + k and source column n; higher bits are zero; some rows are empty. `adjacency_two`: bit k, k below 16, of word (w, n) is the entry of seed row 16 w + k and source column n; higher bits are zero; some rows are empty.
All inputs are finite; a program needn't handle non-finite values.
Results may differ from a plain program's by a relative error of at most 0.0041.
Values may be sent and summed in bfloat16 or wider, within the bound.
No kernel may reach another device: no remote copies, remote signals or barrier semaphores. Data moves between devices by JAX's collectives and lax.ppermute only.
A program may use at most 128 MiB of HBM per device.

v0:
```python
import math
import jax
import jax.numpy as jnp
from jax import lax
from jax.sharding import PartitionSpec as P


def unpack(packed):
    shifts = jnp.arange(16, dtype=jnp.int32)
    spread = jnp.bitwise_and(jnp.right_shift(packed[..., None, :], shifts[:, None]), 1)
    dense = spread.reshape(packed.shape[:-2] + (packed.shape[-2] * 16, packed.shape[-1]))
    degree = jnp.sum(dense, axis=-1).astype(jnp.float32)
    return (dense.astype(jnp.bfloat16), 1.0 / jnp.maximum(degree, 1.0))


def upper_layer(pre_rows, words_two, grad_rows, weight_two, factor):
    hidden = jnp.maximum(pre_rows, 0)
    seed_count = grad_rows.shape[0]
    matrix, inverse = unpack(words_two)
    mixed = (
        jnp.einsum("rsd,dh->rsh", matrix, hidden, preferred_element_type=jnp.float32)
        * inverse[..., None]
    ).astype(jnp.bfloat16)
    scaled = grad_rows.astype(jnp.float32) * factor
    scaled_low = scaled.astype(jnp.bfloat16)
    grad_rel = jnp.einsum("rsh,sk->rhk", mixed, scaled_low, preferred_element_type=jnp.float32)
    grad_self = jnp.einsum(
        "sh,sk->hk", hidden[:seed_count], scaled_low, preferred_element_type=jnp.float32
    )
    weight_grad = jnp.concatenate([grad_self[None], grad_rel], 0)
    backed = (
        jnp.einsum("sk,rhk->rsh", scaled_low, weight_two[1:], preferred_element_type=jnp.float32)
        * inverse[..., None]
    ).astype(jnp.bfloat16)
    spread_back = jnp.einsum("rsd,rsh->dh", matrix, backed, preferred_element_type=jnp.float32)
    own_part = jnp.einsum(
        "sk,hk->sh", scaled_low, weight_two[0], preferred_element_type=jnp.float32
    )
    hidden_total = spread_back + jnp.pad(own_part, ((0, hidden.shape[0] - seed_count), (0, 0)))
    hidden_grad = jnp.where(pre_rows > 0, hidden_total, 0.0).astype(jnp.bfloat16)
    return (
        weight_grad,
        jnp.sum(scaled, 0),
        hidden_grad,
        jnp.sum(hidden_grad.astype(jnp.float32), 0),
    )


def panel_terms(word_block, column_block, grad_block):
    matrix, inverse = unpack(word_block)
    rows_one = grad_block.shape[1]
    gathered = (
        jnp.einsum("brdn,bcn->brdc", matrix, column_block, preferred_element_type=jnp.float32)
        * inverse[..., None]
    ).astype(jnp.bfloat16)
    panel_rel = jnp.einsum(
        "brdc,bdh->rch", gathered, grad_block, preferred_element_type=jnp.float32
    )
    panel_self = jnp.einsum(
        "bcd,bdh->ch", column_block[:, :, :rows_one], grad_block, preferred_element_type=jnp.float32
    )
    return jnp.concatenate([panel_self[None], panel_rel], 0)


def on_device(features, adjacency_one, pre_hidden, adjacency_two, weight_two, out_grad):
    seed_count = out_grad.shape[2]
    factor = float(seed_count * lax.axis_size("feat") * lax.axis_size("rep")) ** (-0.5)
    weight_grad, bias_two, hidden_grad, bias_one = upper_layer(
        pre_hidden[0, 0], adjacency_two[0, 0], out_grad[0, 0], weight_two, factor
    )
    feature_local = features[0]
    adj_local = adjacency_one[0]
    col_width = feature_local.shape[1]
    hidden_width = hidden_grad.shape[1]
    relations = adj_local.shape[1]
    initial = jnp.zeros((relations + 1, col_width, hidden_width), jnp.float32)
    piece = lax.all_gather(hidden_grad[None], "feat", axis=0, tiled=True)
    piece_rows = piece.shape[0]
    group_size = math.gcd(piece_rows, 8)
    turn_count = piece_rows // group_size
    word_block = adj_local
    word_block = word_block.reshape((turn_count, group_size) + adj_local.shape[1:])
    column_block = feature_local
    column_block = column_block.reshape((turn_count, group_size) + feature_local.shape[1:])
    grad_block = piece.reshape((turn_count, group_size) + piece.shape[1:])

    def one_turn(running, inputs):
        return (running + panel_terms(inputs[0], inputs[1], inputs[2]), None)

    running, unused = lax.scan(one_turn, initial, (word_block, column_block, grad_block))
    grad_w1 = lax.psum(running, "rep")
    grad_w2, grad_b1, grad_b2 = lax.psum((weight_grad, bias_one, bias_two), ("feat", "rep"))
    return (grad_w1, grad_b1, grad_w2, grad_b2)


def solution(mesh):
    placed = (
        P("rep", None, "feat", None),
        P("rep", None, None, None, None),
        P("rep", "feat", None, None),
        P("rep", "feat", None, None, None),
        P(),
        P("rep", "feat", None, None),
    )
    return jax.shard_map(
        on_device,
        mesh=mesh,
        in_specs=placed,
        out_specs=(P(None, "feat", None), P(), P(), P()),
        check_vma=False,
    )
```

profile of v0, /device:TPU:0, one launch (start us, length us, event | category | flops | bytes accessed | tf_op | source)
XLA Modules:
  0.0 213.1 jit_solution(5158156742498113044)
XLA Ops:
  8.1 1.6 fusion.28
  9.8 0.1 shift_right_arithmetic.72
  9.9 0.9 fusion.27
  10.8 1.1 fusion.37
  11.9 2.4 %convert_reduce_fusion = (f32[256]{0:T(256)S(1)}, bf16[256,256]{1,0:T(8,128)(2,1)}) fusion(f32[128,256]{1,0:T(8,128)S(1)} %fusion.37, bf16[5,128,256]{2,1,0:T(8,128)(2,1)S(1)} %fusion.27, bf16[6,256,256]{2,1,0:T(8,128)(2,1)} %param.10, f32[5,128]{1,0:T(8,128)S(1)} %div.22, bf16[1,1,128,256]{3,2,1,0:T(8,128)(2,1)} %param.11, bf16[1,1,256,256]{3,2,1,0:T(8,128)(2,1)} %param.8), kind=kOutput, calls=%fused_computation.38 | convolution fusion | flops 168722176 | bytes 1445376 | tf_op jit(solution)/shard_map/rsd,rsh->dh/dot_general | solution.py:35
  14.4 0.9 broadcast_maximum_fusion
  15.4 1.0 convolution_bitcast_fusion.1
  16.4 1.6 fusion.19
  18.0 1.2 pad_maximum_fusion
  19.3 0.2 all-reduce.5.cloned.1.call-start
  19.5 10.9 %and_reduce_fusion = s32[8,5,16,16]{3,2,1,0:T(8,128)S(1)} fusion(s32[8,5,16,512]{3,2,1,0:T(8,128)S(1)} %bitcast.90), kind=kLoop, calls=%fused_computation.3 | loop fusion | flops 15718400 | bytes 1351680 | tf_op jit(solution)/shard_map/while/body/eval_jaxpr/reduce_sum | solution.py:12
  30.5 0.2 reshape.90
  30.7 0.1 shift_right_arithmetic.81
  30.7 10.1 %all-gather.3.cloned.1.call-done = bf16[2048,256]{1,0:T(8,128)(2,1)} async-done(((bf16[256,256]{1,0:T(8,128)(2,1)}), bf16[2048,256]{1,0:T(8,128)(2,1)}) %all-gather.3.cloned.1.call-update) | async-done | bytes 1048592 | tf_op jit(solution)/shard_map/all_gather | solution.py:77
  40.9 10.5 %shift_right_arithmetic.78 = s32[8,5,16,16,512]{4,3,2,1,0:T(8,128)} broadcast(s32[8,5,16,512]{3,2,1,0:T(8,128)S(1)} %bitcast.91), dimensions={0,1,2,4} | broadcast | bytes 22282240 | tf_op jit(solution)/shard_map/while/body/eval_jaxpr/shift_right_arithmetic | solution.py:10
  51.3 9.5 %fusion.13 = f32[5,128,256]{2,1,0:T(8,128)S(1)} fusion(bf16[8,256,256,1]{2,1,0,3:T(8,128)(2,1)S(1)} %bitcast.96, f32[8,5,256]{2,0,1:T(8,128)S(1)} %copy.37, s32[8,5,256,512]{3,2,1,0:T(8,128)} %bitcast.89, s32[256]{0:T(256)S(1)} %shift_right_arithmetic.81, bf16[1,8,128,512]{3,2,1,0:T(8,128)(2,1)S(1)} %copy-done.2), kind=kOutput, calls=%fused_computation.14 | convolution fusion | flops 2031616000 | bytes 23766016 | tf_op jit(solution)/shard_map/while/body/eval_jaxpr/brdc,bdh->rch/dot_general | solution.py:56
  60.8 0.5 convolution_bitcast_fusion.2
  61.3 0.1 copy.30
  61.4 1.0 pad_maximum_fusion.1
  62.4 39.3 %all-reduce.1 = (f32[256]{0:T(256)}, f32[256]{0:T(256)}) all-reduce(f32[256]{0:T(256)S(1)} %get-tuple-element.23, f32[256]{0:T(256)S(1)} %fusion.40), channel_id=1, replica_groups=mesh['feat'=8,'rep'=4] {'feat','rep'}, use_global_device_ids=true, to_apply=%region_4.5 | all-reduce | flops 512 | bytes 4096 | tf_op jit(solution)/shard_map/psum | solution.py:92
  101.8 53.7 %all-reduce.7.cloned.1.call-done = f32[6,256,256]{2,1,0:T(8,128)} async-done(((f32[6,256,256]{2,1,0:T(8,128)}), f32[6,256,256]{2,1,0:T(8,128)}) %all-reduce.7.cloned.1.call-update) | async-done | bytes 1572880 | tf_op jit(solution)/shard_map/psum | solution.py:92
  155.4 45.4 %all-reduce.5.cloned.1.call-done = f32[6,128,256]{2,1,0:T(8,128)} async-done(((f32[6,128,256]{2,1,0:T(8,128)}), f32[6,128,256]{2,1,0:T(8,128)}) %all-reduce.5.cloned.1.call-update) | async-done | bytes 786448 | tf_op jit(solution)/shard_map/psum | solution.py:91
  200.8 2.1 copy.52
  202.9 2.7 %copy.53 = f32[6,256,256]{2,1,0:T(8,128)} copy(f32[6,256,256]{2,1,0:T(8,128)} %all-reduce.7.cloned.1.call-done) | data formatting | bytes 3145728
  (20 shorter events, 0.3 us)
Async XLA Ops:
  8.0 11.5 %copy-start = (s32[1,8,5,16,512]{4,3,2,1,0:T(8,128)S(1)}, s32[1,8,5,16,512]{4,3,2,1,0:T(8,128)}, u32[]{:S(2)}) copy-start(s32[1,8,5,16,512]{4,3,2,1,0:T(8,128)} %param.7) | copy-start | bytes 3932164
  8.0 32.9 %all-gather.3.cloned.1.call-start = ((), (), s32[]{:S(2)}) async-start(), calls=%async_computation.2 | async-start | bytes 1179648 | tf_op jit(solution)/shard_map/all_gather | solution.py:77
  14.4 141.0 %all-reduce.7.cloned.1.call-start = ((), (), s32[]{:S(2)}) async-start(), calls=%async_computation.1 | async-start | bytes 3145728 | tf_op jit(solution)/shard_map/psum | solution.py:92
  19.3 181.5 %all-reduce.5.cloned.1.call-start = ((), (), s32[]{:S(2)}) async-start(), calls=%async_computation | async-start | bytes 1572864 | tf_op jit(solution)/shard_map/psum | solution.py:91
  40.9 10.5 %copy-start.2 = (bf16[1,8,128,512]{3,2,1,0:T(8,128)(2,1)S(1)}, bf16[1,8,128,512]{3,2,1,0:T(8,128)(2,1)}, u32[]{:S(2)}) copy-start(bf16[1,8,128,512]{3,2,1,0:T(8,128)(2,1)} %param.6) | copy-start | bytes 3145732
  40.9 10.5 %copy-start.3 = (bf16[2048,256]{1,0:T(8,128)(2,1)S(1)}, bf16[2048,256]{1,0:T(8,128)(2,1)}, u32[]{:S(2)}) copy-start(bf16[2048,256]{1,0:T(8,128)(2,1)} %all-gather.3.cloned.1.call-done) | copy-start | bytes 3145732
  51.3 11.0 %copy-start.1 = (bf16[1,1,128,256]{3,2,1,0:T(8,128)(2,1)S(1)}, bf16[1,1,128,256]{3,2,1,0:T(8,128)(2,1)}, u32[]{:S(2)}) copy-start(bf16[1,1,128,256]{3,2,1,0:T(8,128)(2,1)} %param.11) | copy-start | bytes 196612
Sparse Core Ops, SparseCore 0:
  14.5 26.3 all-gather.2
Sparse Core Ops, SparseCore 1:
  20.7 134.6 all-reduce.6
  158.2 42.5 all-reduce.4
where the time goes:
time: 214 us; the launch traced here: 213 us
  waiting for transfers between devices  109 us (51%)
  blocking collectives  39.3 us (18%)
  other arithmetic  16.6 us (8%)
  matrix products  16.1 us (8%)
  local copies, waits for them, and re-layouts  15.8 us (7%)
  between operations  15.6 us (7%)
    psum x1, waiting for transfers between devices, on_device(): lax.psum((weight_grad, bias_one, bias_two), ('feat', 'rep'))  53.7 us
    psum x1, waiting for transfers between devices, on_device(): grad_w1 = lax.psum(running, 'rep')  45.4 us
    psum x1, blocking collectives, on_device(): lax.psum((weight_grad, bias_one, bias_two), ('feat', 'rep'))  39.3 us
    reduce_sum x1, other arithmetic, unpack(): degree = jnp.sum(dense, axis=-1).astype(jnp.float32)  10.9 us
    shift_right_arithmetic x5, local copies, waits for them, and re-layouts, unpack(): jnp.right_shift(packed[..., None, :], shifts[:, None])  10.6 us
    all_gather x1, waiting for transfers between devices, on_device(): piece = lax.all_gather(hidden_grad[None], 'feat', axis=0, tiled=True)  10.1 us
    dot_general x1, matrix products, panel_terms(): jnp.einsum('brdc,bdh->rch', gathered, grad_block, preferred_element_type=...  9.46 us
    unnamed x10, local copies, waits for them, and re-layouts  4.85 us
  transfers between devices with their start and end apart: 3, of which 3 were waited for; matrix products, arithmetic and copies ran while one was open for 18% of the time, Pallas kernels for 0%

commit v1 on v0

--- a/solution.py
+++ b/solution.py
@@ -88,7 +88,9 @@
         return (running + panel_terms(inputs[0], inputs[1], inputs[2]), None)
 
     running, unused = lax.scan(one_turn, initial, (word_block, column_block, grad_block))
-    grad_w1 = lax.psum(running, "rep")
+    grad_w1 = running
+    for hop in (1, 2):
+        grad_w1 = grad_w1 + lax.ppermute(grad_w1, "rep", [(dev, dev ^ hop) for dev in range(4)])
     grad_w2, grad_b1, grad_b2 = lax.psum((weight_grad, bias_one, bias_two), ("feat", "rep"))
     return (grad_w1, grad_b1, grad_w2, grad_b2)
 

time: 214 us -> 243 us (1.14)
  blocking collectives: 39.3 us -> 61.3 us
  starting transfers between devices: 0.31 us -> 4.03 us
  waiting for transfers between devices: 109 us -> 112 us
  other arithmetic: 16.6 us -> 19.3 us
    psum x1 -> x0, waiting for transfers between devices: 45.4 us -> none  [on_device(): grad_w1 = lax.psum(running, 'rep')]
    psum x1, waiting for transfers between devices: 53.7 us -> 80.4 us  [on_device(): lax.psum((weight_grad, bias_one, bias_two), ('feat', 'rep'))]
    psum x1, blocking collectives: 39.3 us -> 61.3 us  [on_device(): lax.psum((weight_grad, bias_one, bias_two), ('feat', 'rep'))]
    ppermute x0 -> x2, waiting for transfers between devices: none -> 17.6 us  [on_device(): lax.ppermute(grad_w1, 'rep', [(dev, dev ^ hop) for dev in range(4)])]
    ppermute x0 -> x2, starting transfers between devices: none -> 3.95 us  [on_device(): lax.ppermute(grad_w1, 'rep', [(dev, dev ^ hop) for dev in range(4)])]
    all_gather x1, waiting for transfers between devices: 10.1 us -> 13.7 us  [on_device(): piece = lax.all_gather(hidden_grad[None], 'feat', axis=0, tiled=True)]
  transfers between devices with their start and end apart: 3 -> 4, of which waited for: 3 -> 3; matrix products, arithmetic and copies ran while one was open for 18% -> 7% of each run, Pallas kernels for 0% -> 0%
where the time goes in v1:
time: 243 us
  waiting for transfers between devices  112 us (46%)
  blocking collectives  61.3 us (25%)
  other arithmetic  19.3 us (8%)
  matrix products  15.9 us (7%)
  between operations  15.6 us (6%)
  local copies, waits for them, and re-layouts  14.8 us (6%)
  starting transfers between devices  4.03 us (2%)
    psum x1, waiting for transfers between devices, on_device(): lax.psum((weight_grad, bias_one, bias_two), ('feat', 'rep'))  80.4 us
    psum x1, blocking collectives, on_device(): lax.psum((weight_grad, bias_one, bias_two), ('feat', 'rep'))  61.3 us
    ppermute x2, waiting for transfers between devices, on_device(): lax.ppermute(grad_w1, 'rep', [(dev, dev ^ hop) for dev in range(4)])  17.6 us
    all_gather x1, waiting for transfers between devices, on_device(): piece = lax.all_gather(hidden_grad[None], 'feat', axis=0, tiled=True)  13.7 us
    reduce_sum x1, other arithmetic, unpack(): degree = jnp.sum(dense, axis=-1).astype(jnp.float32)  12.2 us
    shift_right_arithmetic x5, local copies, waits for them, and re-layouts, unpack(): jnp.right_shift(packed[..., None, :], shifts[:, None])  11.7 us
    dot_general x1, matrix products, panel_terms(): jnp.einsum('brdc,bdh->rch', gathered, grad_block, preferred_element_type=...  9.39 us
  transfers between devices with their start and end apart: 4, of which 3 were waited for; matrix products, arithmetic and copies ran while one was open for 7% of the time, Pallas kernels for 0%

profile of v1, /device:TPU:0, one launch (start us, length us, event | category | flops | bytes accessed | tf_op | source)
XLA Modules:
  0.0 242.5 jit_solution(12300111847863722914)
XLA Ops:
  8.0 1.5 fusion.28
  9.7 0.1 shift_right_arithmetic.72
  9.8 0.9 fusion.27
  10.7 1.1 fusion.37
  11.8 2.4 convert_reduce_fusion
  14.3 12.2 %and_reduce_fusion = s32[8,5,16,16]{3,2,1,0:T(8,128)S(1)} fusion(s32[8,5,16,512]{3,2,1,0:T(8,128)} %bitcast.90), kind=kLoop, calls=%fused_computation.3 | loop fusion | flops 15718400 | bytes 1351680 | tf_op jit(solution)/shard_map/while/body/eval_jaxpr/reduce_sum | solution.py:12
  26.6 0.2 reshape.90
  26.9 13.7 %all-gather.3.cloned.1.call-done = bf16[2048,256]{1,0:T(8,128)(2,1)} async-done(((bf16[256,256]{1,0:T(8,128)(2,1)}), bf16[2048,256]{1,0:T(8,128)(2,1)}) %all-gather.3.cloned.1.call-update) | async-done | bytes 1048592 | tf_op jit(solution)/shard_map/all_gather | solution.py:77
  40.5 2.0 convolution_bitcast_fusion.2
  42.5 0.1 copy.30
  42.7 11.5 %shift_right_arithmetic.78 = s32[8,5,16,16,512]{4,3,2,1,0:T(8,128)} broadcast(s32[8,5,16,512]{3,2,1,0:T(8,128)} %bitcast.91), dimensions={0,1,2,4} | broadcast | bytes 22282240 | tf_op jit(solution)/shard_map/while/body/eval_jaxpr/shift_right_arithmetic | solution.py:10
  54.2 9.4 %fusion.13 = f32[5,128,256]{2,1,0:T(8,128)S(1)} fusion(bf16[8,256,256,1]{2,1,0,3:T(8,128)(2,1)} %bitcast.97, f32[8,5,256]{2,0,1:T(8,128)S(1)} %copy.37, s32[8,5,256,512]{3,2,1,0:T(8,128)} %bitcast.89, s32[256]{0:T(256)S(1)} %shift_right_arithmetic.81, bf16[1,8,128,512]{3,2,1,0:T(8,128)(2,1)S(1)} %copy-done.2), kind=kOutput, calls=%fused_computation.14 | convolution fusion | flops 2031616000 | bytes 23766016 | tf_op jit(solution)/shard_map/while/body/eval_jaxpr/brdc,bdh->rch/dot_general | solution.py:56
  63.6 1.0 pad_maximum_fusion.1
  64.6 1.5 collective-permute-start
  66.1 0.2 convolution_bitcast_fusion.1
  66.3 0.7 fusion.19
  67.0 17.6 %collective-permute-done = f32[6,128,256]{2,1,0:T(8,128)} collective-permute-done((f32[6,128,256]{2,1,0:T(8,128)}, f32[6,128,256]{2,1,0:T(8,128)}, u32[]{:S(2)}, u32[]{:S(2)}) %collective-permute-start) | collective-permute-done | bytes 786464 | tf_op jit(solution)/shard_map/ppermute | solution.py:93
  84.6 1.3 fusion.59
  85.8 2.5 %collective-permute-start.1 = (f32[6,128,256]{2,1,0:T(8,128)S(1)}, f32[6,128,256]{2,1,0:T(8,128)S(1)}, u32[]{:S(2)}, u32[]{:S(2)}) collective-permute-start(f32[6,128,256]{2,1,0:T(8,128)S(1)} %fusion.59), channel_id=1, source_target_pairs={{0,2},{1,3},{2,0},{3,1},{4,6},{5,7},{6,4},{7,5},{8,10},{9,11},{10,... | collective-permute-start | bytes 2359304 | tf_op jit(solution)/shard_map/ppermute | solution.py:93
  88.3 1.3 pad_maximum_fusion
  89.7 61.3 %all-reduce.1 = (f32[256]{0:T(256)}, f32[256]{0:T(256)}) all-reduce(f32[256]{0:T(256)S(1)} %get-tuple-element.23, f32[256]{0:T(256)S(1)} %fusion.40), channel_id=1, replica_groups=mesh['feat'=8,'rep'=4] {'feat','rep'}, use_global_device_ids=true, to_apply=%region_3.4 | all-reduce | flops 512 | bytes 4096 | tf_op jit(solution)/shard_map/psum | solution.py:94
  151.0 1.0 add.23
  152.0 80.4 %all-reduce.4.cloned.1.call-done = f32[6,256,256]{2,1,0:T(8,128)} async-done(((f32[6,256,256]{2,1,0:T(8,128)}), f32[6,256,256]{2,1,0:T(8,128)}) %all-reduce.4.cloned.1.call-update) | async-done | bytes 1572880 | tf_op jit(solution)/shard_map/psum | solution.py:94
  232.3 2.7 %copy.51 = f32[6,256,256]{2,1,0:T(8,128)} copy(f32[6,256,256]{2,1,0:T(8,128)} %all-reduce.4.cloned.1.call-done) | data formatting | bytes 3145728
  (20 shorter events, 0.4 us)
Async XLA Ops:
  8.0 32.5 %all-gather.3.cloned.1.call-start = ((), (), s32[]{:S(2)}) async-start(), calls=%async_computation.1 | async-start | bytes 1179648 | tf_op jit(solution)/shard_map/all_gather | solution.py:77
  14.3 218.1 %all-reduce.4.cloned.1.call-start = ((), (), s32[]{:S(2)}) async-start(), calls=%async_computation | async-start | bytes 3145728 | tf_op jit(solution)/shard_map/psum | solution.py:94
  42.7 11.5 %copy-start.2 = (bf16[1,8,128,512]{3,2,1,0:T(8,128)(2,1)S(1)}, bf16[1,8,128,512]{3,2,1,0:T(8,128)(2,1)}, u32[]{:S(2)}) copy-start(bf16[1,8,128,512]{3,2,1,0:T(8,128)(2,1)} %param.6) | copy-start | bytes 3145732
  54.2 11.9 %copy-start.1 = (bf16[1,1,256,256]{3,2,1,0:T(8,128)(2,1)S(1)}, bf16[1,1,256,256]{3,2,1,0:T(8,128)(2,1)}, u32[]{:S(2)}) copy-start(bf16[1,1,256,256]{3,2,1,0:T(8,128)(2,1)} %param.8) | copy-start | bytes 393220
  54.2 11.9 %copy-start = (bf16[1,1,128,256]{3,2,1,0:T(8,128)(2,1)S(1)}, bf16[1,1,128,256]{3,2,1,0:T(8,128)(2,1)}, u32[]{:S(2)}) copy-start(bf16[1,1,128,256]{3,2,1,0:T(8,128)(2,1)} %param.11) | copy-start | bytes 196612
  64.6 20.0 %collective-permute-start = (f32[6,128,256]{2,1,0:T(8,128)}, f32[6,128,256]{2,1,0:T(8,128)}, u32[]{:S(2)}, u32[]{:S(2)}) collective-permute-start(f32[6,128,256]{2,1,0:T(8,128)} %pad_maximum_fusion.1), channel_id=1, source_target_pairs={{0,1},{1,0},{2,3},{3,2},{4,5},{5,4},{6,7},{7,6},{8,9},{9,8},{10,11... | collective-permute-start | bytes 2359304 | tf_op jit(solution)/shard_map/ppermute | solution.py:93
  85.8 65.1 %collective-permute-start.1 = (f32[6,128,256]{2,1,0:T(8,128)S(1)}, f32[6,128,256]{2,1,0:T(8,128)S(1)}, u32[]{:S(2)}, u32[]{:S(2)}) collective-permute-start(f32[6,128,256]{2,1,0:T(8,128)S(1)} %fusion.59), channel_id=1, source_target_pairs={{0,2},{1,3},{2,0},{3,1},{4,6},{5,7},{6,4},{7,5},{8,10},{9,11},{10,... | collective-permute-start | bytes 2359304 | tf_op jit(solution)/shard_map/ppermute | solution.py:93
Sparse Core Ops, SparseCore 0:
  14.4 26.0 all-gather.2
Sparse Core Ops, SparseCore 1:
  89.7 142.5 all-reduce.3
